TPU v7x, 256 devices: a whole 4x4x8 slice. The times are simulated.
256 devices in a mesh: cfg: 64 (over z, x_lo, y), lat: 4 (over x_hi, core).
Axes of the slice: x: 4 (x_hi: 2, x_lo: 2; x = x_hi * 2 + x_lo), y: 4, z: 8, core: 2. Of those that a mesh axis runs over, the one named last changes fastest.
Arguments:
- latent_mode: float32 [128, 1048576], P('cfg', 'lat'), may hold values from -6 to 6
- latent_var: float32 [128, 1048576], P('cfg', 'lat'), may hold values from 0.05 to 2
- config_weight: float32 [128], P('cfg'), may hold values from 0.05 to 20
- grid_offset: float32 [64], replicated, may hold values from -3 to 3
Outputs:
- marginal_density: float32 [64, 1048576], P(None, ('cfg', 'lat'))
- marginal_moments: float32 [2, 1048576], P(None, ('cfg', 'lat'))
All inputs are finite; a program needn't handle non-finite values.
Results may differ from a plain program's by a relative error of at most 0.00002.
Values sent between devices are 32-bit elements; how exact they have to be, the bound alone decides.
No kernel may reach another device: no remote copies, remote signals or barrier semaphores. Data moves between devices by JAX's collectives and lax.ppermute only.
A program may use at most 64 MiB of HBM per device.

v0:
```python
import jax
import jax.numpy as jnp
from jax import lax
from jax.experimental import pallas as pl
from jax.experimental.pallas import tpu as pltpu
from jax.sharding import PartitionSpec as P


LANES = 128
SUB = 8
BLOCK_ROWS = 64
ROWS_A = 36
PITCH_A = 2 * ROWS_A + 1
UNROLL = 32
LOG2E = 1.4426950408889634
TWO_PI = 6.283185307179586
F32 = jnp.float32
VMEM = pl.BlockSpec(memory_space=pltpu.VMEM)
SMEM = pl.BlockSpec(memory_space=pltpu.SMEM)
HBM = pl.BlockSpec(memory_space=pl.ANY)


def rows_of(array):
    own_cfg, width = array.shape
    rows = array.reshape(own_cfg, width // LANES, LANES).transpose(1, 0, 2)
    return rows.reshape(16, 4, BLOCK_ROWS, LANES)


def held_at(z, lat):
    d = (lat - z) & 3
    return 2 * (d & 1) + (d >> 1)


def pack_first_kernel(mode, var, weight, out, held, in_sems, out_sems):
    lat = lax.axis_index("lat")
    arrive, leave = [], []
    for z in range(4):
        here = []
        for a, array in enumerate((mode, var)):
            src = array.at[:, held_at(z, lat), pl.ds(0, ROWS_A)]
            dst = held.at[pl.ds(16 * z, 16), pl.ds(a * ROWS_A, ROWS_A)]
            here.append(pltpu.make_async_copy(src, dst, in_sems.at[2 * z + a]))
        arrive.append(here)
        at = pl.ds(16 * z, 16)
        leave.append(pltpu.make_async_copy(held.at[at], out.at[at], out_sems.at[z]))
    for here in arrive:
        for c in here:
            c.start()
    lane = lax.broadcasted_iota(jnp.int32, (1, LANES), 1)
    row = jnp.where(lane < LANES // 2, jnp.full((1, LANES), weight[0], F32), jnp.full((1, LANES), weight[1], F32))
    for c in range(64):
        held[c, 2 * ROWS_A] = row
    for here, go in zip(arrive, leave):
        for c in here:
            c.wait()
        go.start()
    for go in leave:
        go.wait()


def pack_first(mode, var, weight):
    shape = (64, PITCH_A, 1, LANES)
    return pl.pallas_call(
        pack_first_kernel,
        out_shape=jax.ShapeDtypeStruct(shape, F32),
        in_specs=[HBM] * 2 + [SMEM],
        out_specs=HBM,
        scratch_shapes=[pltpu.VMEM(shape, F32), pltpu.SemaphoreType.DMA((8,)), pltpu.SemaphoreType.DMA((4,))],
        name="pack_first",
    )(mode[:, :, :, None, :], var[:, :, :, None, :], weight)


def pack_second_kernel(mode, var, b0, b1, b2, b3, h0, h1, h2, h3, in_sems, out_sems):
    lat = lax.axis_index("lat")
    rest = BLOCK_ROWS - ROWS_A
    arrive, leave = [], []
    for r, piece, held in ((3, b3, h3), (2, b2, h2), (1, b1, h1), (0, b0, h0)):
        here = []
        for a, array in enumerate((mode, var)):
            src = array.at[:, jnp.bitwise_xor(lat, r), pl.ds(ROWS_A, rest)]
            here.append(pltpu.make_async_copy(src, held.at[:, pl.ds(a * rest, rest)], in_sems.at[2 * r + a]))
        arrive.append(here)
        leave.append(pltpu.make_async_copy(held, piece, out_sems.at[r]))
    for here in arrive:
        for c in here:
            c.start()
    for here, go in zip(arrive, leave):
        for c in here:
            c.wait()
        go.start()
    for go in leave:
        go.wait()


def pack_second(mode, var):
    shape = (16, 2 * (BLOCK_ROWS - ROWS_A), 1, LANES)
    return pl.pallas_call(
        pack_second_kernel,
        out_shape=(jax.ShapeDtypeStruct(shape, F32),) * 4,
        in_specs=[HBM] * 2,
        out_specs=[HBM] * 4,
        scratch_shapes=[pltpu.VMEM(shape, F32)] * 4 + [pltpu.SemaphoreType.DMA((8,)), pltpu.SemaphoreType.DMA((4,))],
        name="pack_second",
    )(mode[:, :, :, None, :], var[:, :, :, None, :])


def merge_kernel(p0, p1, p2, p3, grid_offset, out, offset, held, in_sems, out_sems):
    lat = lax.axis_index("lat")
    arrive, leave = [], []
    for r, piece in enumerate((p0, p1, p2, p3)):
        at = pl.ds(16 * jnp.bitwise_xor(lat, r), 16)
        arrive.append(pltpu.make_async_copy(piece, held.at[r], in_sems.at[r]))
        leave.append(pltpu.make_async_copy(held.at[r], out.at[at], out_sems.at[r]))
    for c in arrive:
        c.start()
    for g in range(64):
        offset[g : g + 1, :] = jnp.full((1, LANES), grid_offset[g], F32)
    for c, go in zip(arrive, leave):
        c.wait()
        go.start()
    for go in leave:
        go.wait()


def merge(pieces, grid_offset):
    rows = pieces[0].shape[1]
    return pl.pallas_call(
        merge_kernel,
        out_shape=(jax.ShapeDtypeStruct((64, rows, 1, LANES), F32), jax.ShapeDtypeStruct((64, LANES), F32)),
        in_specs=[HBM] * 4 + [SMEM],
        out_specs=[HBM, VMEM],
        scratch_shapes=[
            pltpu.VMEM((4, 16, rows, 1, LANES), F32),
            pltpu.SemaphoreType.DMA((4,)),
            pltpu.SemaphoreType.DMA((4,)),
        ],
        name="merge",
    )(*pieces, grid_offset)


def prepare(rows, load, norm, modes, precs, logs, centres, spreads):
    groups = rows // 2
    zero = jnp.zeros((SUB, LANES), F32)
    for n, base in enumerate(starts_of(groups)):
        at = slice(SUB * n, SUB * (n + 1))

        def centre_step(i, sums, base=base, at=at):
            new = []
            for u in range(4):
                c = 4 * i + u
                for k in range(2):
                    m = load(c, 2 * base + k)
                    modes[2 * c + k, at, :] = m
                    new.append(norm[pl.ds(2 * c + k, SUB, stride=0), :] * m)
            return tuple(s + (new[2 * n] + new[2 * n + 1]) for n, s in enumerate(sums))

        s = lax.fori_loop(0, 16, centre_step, (zero,) * 4)
        centre = (s[0] + s[1]) + (s[2] + s[3])

        def spread_step(i, sums, base=base, at=at, centre=centre):
            new = []
            for u in range(4):
                c = 4 * i + u
                for k in range(2):
                    v = load(c, rows + 2 * base + k)
                    w = norm[pl.ds(2 * c + k, SUB, stride=0), :]
                    d = modes[2 * c + k, at, :] - centre
                    new.append(w * (v + d * d))
                    inverse = 1.0 / v
                    precs[2 * c + k, at, :] = (-0.5 * LOG2E) * inverse
                    logs[2 * c + k, at, :] = 0.5 * jnp.log2((w * w) * (1.0 / TWO_PI) * inverse)
            return tuple(s + (new[2 * n] + new[2 * n + 1]) for n, s in enumerate(sums))

        s = lax.fori_loop(0, 16, spread_step, (zero,) * 4)
        centres[at, :] = centre
        spreads[at, :] = jnp.sqrt((s[0] + s[1]) + (s[2] + s[3]))


def starts_of(groups):
    return [min(SUB * n, groups - SUB) for n in range(-(-groups // SUB))]


def row_of(group, groups):
    last = groups - groups % SUB
    return group if last == groups else jnp.where(group < last, group, group + SUB - groups % SUB)


def densities(groups, offset, modes, precs, logs, centres, spreads, put, done=lambda q: None):
    def pair(q, _):
        rows = [row_of(2 * q + n, groups) for n in range(2)]
        spread = [spreads[pl.ds(r, SUB, stride=0), :] for r in rows]
        centre = [centres[pl.ds(r, SUB, stride=0), :] for r in rows]
        points = [[c + offset[SUB * b : SUB * (b + 1), :] * s for b in range(8)] for c, s in zip(centre, spread)]

        def config_step(k, sums):
            out = []
            for n, r in enumerate(rows):
                m, p, lc = (ref[k, pl.ds(r, SUB, stride=0), :] for ref in (modes, precs, logs))
                for b in range(8):
                    gap = points[n][b] - m
                    out.append(sums[8 * n + b] + jnp.exp2(lc + p * (gap * gap)))
            return tuple(out)

        sums = lax.fori_loop(0, 128, config_step, (jnp.zeros((SUB, LANES), F32),) * 16, unroll=UNROLL)
        for n in range(2):
            put(2 * q + n, [sums[8 * n + b] * spread[n] for b in range(8)])
        done(q)
        return 0

    lax.fori_loop(0, groups // 2, pair, 0)


def normalise(data, norm):
    lane = lax.broadcasted_iota(jnp.int32, (1, LANES), 1)
    rows = [data[PITCH_A * c + 2 * ROWS_A : PITCH_A * c + 2 * ROWS_A + 1, :] for c in range(64)]
    rows = [(jnp.where(lane < 1, r, 0.0), jnp.where(lane == LANES - 1, r, 0.0)) for r in rows]
    rows = [jnp.sum(r, axis=1, keepdims=True) for pair in rows for r in pair]
    total = rows
    while len(total) > 1:
        total = [a + b for a, b in zip(total[::2], total[1::2])]
    inverse = 1.0 / total[0]
    for k, r in enumerate(rows):
        norm[k : k + 1, :] = jnp.broadcast_to(r * inverse, (1, LANES))


def first_kernel(data, offset, out, norm, modes, precs, logs, centres, spreads):
    groups = ROWS_A // 2
    normalise(data, norm)

    def load(c, row):
        return data[pl.ds(PITCH_A * c + row, SUB, stride=2), :]

    prepare(ROWS_A, load, norm, modes, precs, logs, centres, spreads)

    def put(group, values):
        for b, value in enumerate(values):
            out[pl.ds(pl.multiple_of(64 * group + SUB * b, SUB), SUB), :] = value

    densities(groups, offset, modes, precs, logs, centres, spreads, put)
    for group in range(groups):
        row = group if group < groups - groups % SUB else group + SUB - groups % SUB
        out[64 * groups + group : 64 * groups + group + 1, :] = centres[row : row + 1, :]
        out[65 * groups + group : 65 * groups + group + 1, :] = spreads[row : row + 1, :]


def second_kernel(
    data, offset, norm, density, moments, modes, precs, logs, centres, spreads, own, own_moments, out_sems
):
    rows = BLOCK_ROWS - ROWS_A
    groups = rows // 2

    def load(c, row):
        return data[pl.ds(2 * rows * c + row, SUB, stride=2), :]

    prepare(rows, load, norm, modes, precs, logs, centres, spreads)
    for group in range(groups):
        row = group if group < groups - groups % SUB else group + SUB - groups % SUB
        own_moments[0:1, group * LANES : (group + 1) * LANES] = centres[row : row + 1, :]
        own_moments[1:2, group * LANES : (group + 1) * LANES] = spreads[row : row + 1, :]
    start = ROWS_A // 2 * LANES
    moments_copy = pltpu.make_async_copy(own_moments, moments.at[:, pl.ds(start, groups * LANES)], out_sems.at[groups // 2])
    moments_copy.start()

    def columns(q):
        at = pl.multiple_of(q * 2 * LANES, 2 * LANES)
        src = own.at[:, pl.ds(at, 2 * LANES)]
        dst = density.at[:, pl.ds(pl.multiple_of(start + at, 2 * LANES), 2 * LANES)]
        return pltpu.make_async_copy(src, dst, out_sems.at[q])

    def put(group, values):
        for b, value in enumerate(values):
            own[SUB * b : SUB * (b + 1), pl.ds(pl.multiple_of(group * LANES, LANES), LANES)] = value

    densities(groups, offset, modes, precs, logs, centres, spreads, put, lambda q: columns(q).start())
    for q in range(groups // 2):
        columns(q).wait()
    moments_copy.wait()


def place_kernel(first, density_in, moments_in, tick, density, moments, held, held_moments, sems):
    groups = ROWS_A // 2
    for j in range(groups):
        at = slice(j * LANES, (j + 1) * LANES)
        held[:, at] = first[64 * j : 64 * (j + 1), :]
        held_moments[0:1, at] = first[64 * groups + j : 64 * groups + j + 1, :]
        held_moments[1:2, at] = first[65 * groups + j : 65 * groups + j + 1, :]
    at = pl.ds(0, groups * LANES)
    copies = [
        pltpu.make_async_copy(held, density.at[:, at], sems.at[0]),
        pltpu.make_async_copy(held_moments, moments.at[:, at], sems.at[1]),
    ]
    for c in copies:
        c.start()
    for c in copies:
        c.wait()


def scratch(groups):
    held = SUB * len(starts_of(groups))
    return [pltpu.VMEM((128, held, LANES), F32)] * 3 + [pltpu.VMEM((held, LANES), F32)] * 2


def cost(groups):
    work = 128 * 64 * groups * LANES
    return pl.CostEstimate(flops=6 * work, transcendentals=work, bytes_accessed=4 * 128 * 2 * groups * LANES)


def first_density(data, offset):
    groups = ROWS_A // 2
    shape = jax.ShapeDtypeStruct
    return pl.pallas_call(
        first_kernel,
        out_shape=(shape((66 * groups, LANES), F32), shape((128, LANES), F32)),
        in_specs=[VMEM, VMEM],
        out_specs=[VMEM] * 2,
        scratch_shapes=scratch(groups),
        cost_estimate=cost(groups),
        name="first_density",
    )(data, offset)


def outputs():
    width = BLOCK_ROWS // 2 * LANES
    return (jax.ShapeDtypeStruct((64, width), F32), jax.ShapeDtypeStruct((2, width), F32))


def staged(groups):
    return [pltpu.VMEM((64, groups * LANES), F32), pltpu.VMEM((2, groups * LANES), F32)]


def second_density(data, offset, norm):
    groups = (BLOCK_ROWS - ROWS_A) // 2
    return pl.pallas_call(
        second_kernel,
        out_shape=outputs(),
        in_specs=[VMEM, VMEM, VMEM],
        out_specs=[HBM] * 2,
        scratch_shapes=scratch(groups)
        + staged(groups)
        + [
            pltpu.SemaphoreType.DMA((groups // 2 + 1,)),
        ],
        cost_estimate=cost(groups),
        name="second_density",
    )(data, offset, norm)


def place(first, density, moments, tick):
    return pl.pallas_call(
        place_kernel,
        out_shape=outputs(),
        in_specs=[VMEM, HBM, HBM, HBM],
        out_specs=[HBM] * 2,
        scratch_shapes=staged(ROWS_A // 2) + [pltpu.SemaphoreType.DMA((2,))],
        input_output_aliases={1: 0, 2: 1},
        name="place",
    )(first, density, moments, tick)


def in_vmem(array):
    return pltpu.with_memory_space_constraint(array, pltpu.VMEM)


def exchanged(parts):
    return lax.all_to_all(parts, "cfg", split_axis=0, concat_axis=0, tiled=True)


def way_home():
    along_x, along_z = [], []
    for z in range(4):
        for c in range(16):
            for l in range(4):
                lat = held_at(z, l)
                along_x.append(((16 * z + c) * 4 + l, (16 * z + c) * 4 + lat))
                along_z.append(((16 * z + c) * 4 + lat, (16 * l + c) * 4 + lat))
    return along_x, along_z


def per_device(latent_mode, latent_var, config_weight, grid_offset):
    mode, var = rows_of(latent_mode), rows_of(latent_var)
    part_a = pack_first(mode, var, config_weight)
    data_a = exchanged(part_a)
    pieces = pack_second(mode, var)
    arrived = [pieces[0]]
    for r in range(1, 4):
        arrived.append(lax.ppermute(pieces[r], "lat", [(l, l ^ r) for l in range(4)]))
    part_b, offset = merge(arrived, grid_offset)
    data_b = exchanged(part_b)
    sums_a, norm = first_density(in_vmem(data_a.reshape(-1, LANES)), offset)
    along_x, along_z = way_home()
    sums_a = lax.ppermute(sums_a, ("cfg", "lat"), along_x)
    tick = lax.ppermute(sums_a[:SUB], "lat", [(l, l ^ 1) for l in range(4)])
    sums_a = lax.ppermute(sums_a, ("cfg", "lat"), along_z)
    density, moments = second_density(in_vmem(data_b.reshape(-1, LANES)), offset, norm)
    density, moments = place(in_vmem(sums_a), density, moments, tick)
    return (density, moments)


def solution(mesh):
    return jax.shard_map(
        per_device,
        mesh=mesh,
        in_specs=(P("cfg", "lat"), P("cfg", "lat"), P("cfg"), P()),
        out_specs=(P(None, ("cfg", "lat")), P(None, ("cfg", "lat"))),
        check_vma=False,
    )
```

profile of v0, /device:TPU:2, one launch (start us, length us, event | category | flops | bytes accessed | tf_op | source)
XLA Modules:
  0.0 144.4 jit_solution(11527709251965502610)
XLA Ops:
  0.6 3.3 %pack_first.1 = f32[64,73,1,128]{3,2,1,0:T(1,128)} custom-call(f32[16,4,64,1,128]{4,3,2,1,0:T(1,128)} %bitcast.13, f32[16,4,64,1,128]{4,3,2,1,0:T(1,128)} %bitcast.15, f32[2]{0:T(128)} %weight.1), custom_call_target="tpu_custom_call" | custom-call | tf_op jit(solution)/shard_map/pack_first/pallas_call | solution.py:63
  3.9 13.1 %all-to-all-start = ((f32[64,73,1,128]{3,2,1,0:T(1,128)}), f32[64,73,1,128]{3,2,1,0:T(1,128)S(1)}, u32[]{:S(2)}, u32[]{:S(2)}) async-start(f32[64,73,1,128]{3,2,1,0:T(1,128)} %pack_first.1), calls=%async_computation | async-start | bytes 4784128 | tf_op jit(solution)/shard_map/all_to_all | solution.py:365
  17.0 2.5 %pack_second.1 = (f32[16,56,1,128]{3,2,1,0:T(1,128)}, f32[16,56,1,128]{3,2,1,0:T(1,128)}, f32[16,56,1,128]{3,2,1,0:T(1,128)}, f32[16,56,1,128]{3,2,1,0:T(1,128)}) custom-call(f32[16,4,64,1,128]{4,3,2,1,0:T(1,128)} %bitcast.14, f32[16,4,64,1,128]{4,3,2,1,0:T(1,128)} %bitcast.16), custom_call_target="tpu_custom_call" | custom-call | tf_op jit(solution)/shard_map/pack_second/pallas_call | solution.py:97
  19.5 0.1 collective-permute-start
  19.6 2.2 %collective-permute-start.1 = (f32[16,56,1,128]{3,2,1,0:T(1,128)}, f32[16,56,1,128]{3,2,1,0:T(1,128)S(1)}, u32[]{:S(2)}, u32[]{:S(2)}) collective-permute-start(f32[16,56,1,128]{3,2,1,0:T(1,128)} %get-tuple-element.14), channel_id=1, source_target_pairs={{0,2},{1,3},{2,0},{3,1},{4,6},{5,7},{6,4},{7,5},{8,10},{9,11},{10,... | collective-permute-start | bytes 1376264 | tf_op jit(solution)/shard_map/ppermute | solution.py:386
  21.8 1.1 collective-permute-start.2
  23.0 0.0 collective-permute-done.p1
  23.0 0.0 copy-start
  23.0 17.6 %collective-permute-done.1.p2 = f32[16,56,1,128]{3,2,1,0:T(1,128)S(1)} collective-permute-done((f32[16,56,1,128]{3,2,1,0:T(1,128)}, f32[16,56,1,128]{3,2,1,0:T(1,128)S(1)}, u32[]{:S(2)}, u32[]{:S(2)}) %collective-permute-start.1) | collective-permute-done | bytes 458784 | tf_op jit(solution)/shard_map/ppermute | solution.py:386
  40.5 0.0 copy-start.1
  40.5 16.7 %collective-permute-done.2.p3 = f32[16,56,1,128]{3,2,1,0:T(1,128)} collective-permute-done((f32[16,56,1,128]{3,2,1,0:T(1,128)}, f32[16,56,1,128]{3,2,1,0:T(1,128)}, u32[]{:S(2)}, u32[]{:S(2)}) %collective-permute-start.2) | collective-permute-done | bytes 458784 | tf_op jit(solution)/shard_map/ppermute | solution.py:386
  57.2 0.0 copy-done
  57.2 0.0 copy-done.1
  57.2 3.6 %merge.1 = (f32[64,56,1,128]{3,2,1,0:T(1,128)}, f32[64,128]{1,0:T(8,128)}) custom-call(f32[16,56,1,128]{3,2,1,0:T(1,128)} %get-tuple-element.12.p0, f32[16,56,1,128]{3,2,1,0:T(1,128)} %copy-done, f32[16,56,1,128]{3,2,1,0:T(1,128)} %copy-done.1, f32[16,56,1,128]{3,2,1,0:T(1,128)} %collective-permute-done.2.p3, f32[64]{0:T(128)} %grid_offset.1), custom_call_target="tpu_custom_call" | custom-call | tf_op jit(solution)/shard_map/merge/pallas_call | solution.py:127
  60.8 12.9 %all-to-all-done = f32[64,73,1,128]{3,2,1,0:T(1,128)S(1)} async-done(((f32[64,73,1,128]{3,2,1,0:T(1,128)}), f32[64,73,1,128]{3,2,1,0:T(1,128)S(1)}, u32[]{:S(2)}, u32[]{:S(2)}) %all-to-all-start) | async-done | bytes 2392096 | tf_op jit(solution)/shard_map/all_to_all | solution.py:365
  73.8 7.0 %all-to-all-start.1 = ((f32[64,56,1,128]{3,2,1,0:T(1,128)}), f32[64,56,1,128]{3,2,1,0:T(1,128)}, u32[]{:S(2)}, u32[]{:S(2)}) async-start(f32[64,56,1,128]{3,2,1,0:T(1,128)} %get-tuple-element.18), calls=%async_computation.1 | async-start | bytes 3670016 | tf_op jit(solution)/shard_map/all_to_all | solution.py:365
  80.8 18.5 %first_density.1 = (f32[1188,128]{1,0:T(8,128)}, f32[128,128]{1,0:T(8,128)}) custom-call(f32[4672,128]{1,0:T(8,128)S(1)} %bitcast.12, f32[64,128]{1,0:T(8,128)} %get-tuple-element.16.offset), custom_call_target="tpu_custom_call" | custom-call | flops 113246208 | bytes 2359296 | tf_op jit(solution)/shard_map/first_density/pallas_call | solution.py:311
  99.3 1.7 %collective-permute-start.3 = (f32[1188,128]{1,0:T(8,128)}, f32[1188,128]{1,0:T(8,128)S(1)}, u32[]{:S(2)}, u32[]{:S(2)}) collective-permute-start(f32[1188,128]{1,0:T(8,128)} %get-tuple-element.17), channel_id=1, source_target_pairs={{0,0},{1,2},{2,1},{3,3},{4,4},{5,6},{6,5},{7,7},{8,8},{9,10},{10,9... | collective-permute-start | bytes 1824776 | tf_op jit(solution)/shard_map/ppermute | solution.py:391
  101.0 0.0 collective-permute-done.3
  101.0 0.7 collective-permute-start.4
  101.7 19.9 %collective-permute-start.5 = (f32[8,128]{1,0:T(8,128)S(1)}, f32[8,128]{1,0:T(8,128)S(1)}, u32[]{:S(2)}, u32[]{:S(2)}) collective-permute-start(f32[8,128]{1,0:T(8,128)S(1)} %slice.4), channel_id=1, source_target_pairs={{0,1},{1,0},{2,3},{3,2},{4,5},{5,4},{6,7},{7,6},{8,9},{9,8},{10,11... | collective-permute-start | bytes 12296 | tf_op jit(solution)/shard_map/ppermute | solution.py:392
  121.6 6.5 %all-to-all-done.1 = f32[64,56,1,128]{3,2,1,0:T(1,128)} async-done(((f32[64,56,1,128]{3,2,1,0:T(1,128)}), f32[64,56,1,128]{3,2,1,0:T(1,128)}, u32[]{:S(2)}, u32[]{:S(2)}) %all-to-all-start.1) | async-done | bytes 1835040 | tf_op jit(solution)/shard_map/all_to_all | solution.py:365
  128.1 14.9 %second_density.1 = (f32[64,4096]{1,0:T(8,128)}, f32[2,4096]{1,0:T(2,128)}) custom-call(f32[3584,128]{1,0:T(8,128)} %bitcast.11.data, f32[64,128]{1,0:T(8,128)} %get-tuple-element.16.offset, f32[128,128]{1,0:T(8,128)} %get-tuple-element.19.norm), custom_call_target="tpu_custom_call" | custom-call | flops 88080384 | bytes 1835008 | tf_op jit(solution)/shard_map/second_density/pallas_call | solution.py:333
  143.0 0.0 collective-permute-done.5.tick
  143.0 0.0 copy-start.2
  143.0 0.0 collective-permute-done.4.first
  143.0 0.6 copy-done.2
  143.6 0.9 place.1
  (1 shorter events, 0.0 us)
Async XLA Ops:
  3.9 69.9 %all-to-all-start = ((f32[64,73,1,128]{3,2,1,0:T(1,128)}), f32[64,73,1,128]{3,2,1,0:T(1,128)S(1)}, u32[]{:S(2)}, u32[]{:S(2)}) async-start(f32[64,73,1,128]{3,2,1,0:T(1,128)} %pack_first.1), calls=%async_computation | async-start | bytes 4784128 | tf_op jit(solution)/shard_map/all_to_all | solution.py:365
  19.5 3.5 %collective-permute-start = (f32[16,56,1,128]{3,2,1,0:T(1,128)}, f32[16,56,1,128]{3,2,1,0:T(1,128)S(1)}, u32[]{:S(2)}, u32[]{:S(2)}) collective-permute-start(f32[16,56,1,128]{3,2,1,0:T(1,128)} %get-tuple-element.13), channel_id=1, source_target_pairs={{0,1},{1,0},{2,3},{3,2},{4,5},{5,4},{6,7},{7,6},{8,9},{9,8},{10,11... | collective-permute-start | bytes 1376264 | tf_op jit(solution)/shard_map/ppermute | solution.py:386
  19.6 20.9 %collective-permute-start.1 = (f32[16,56,1,128]{3,2,1,0:T(1,128)}, f32[16,56,1,128]{3,2,1,0:T(1,128)S(1)}, u32[]{:S(2)}, u32[]{:S(2)}) collective-permute-start(f32[16,56,1,128]{3,2,1,0:T(1,128)} %get-tuple-element.14), channel_id=1, source_target_pairs={{0,2},{1,3},{2,0},{3,1},{4,6},{5,7},{6,4},{7,5},{8,10},{9,11},{10,... | collective-permute-start | bytes 1376264 | tf_op jit(solution)/shard_map/ppermute | solution.py:386
  21.8 35.4 %collective-permute-start.2 = (f32[16,56,1,128]{3,2,1,0:T(1,128)}, f32[16,56,1,128]{3,2,1,0:T(1,128)}, u32[]{:S(2)}, u32[]{:S(2)}) collective-permute-start(f32[16,56,1,128]{3,2,1,0:T(1,128)} %get-tuple-element.15), channel_id=1, source_target_pairs={{0,3},{1,2},{2,1},{3,0},{4,7},{5,6},{6,5},{7,4},{8,11},{9,10},{10,... | collective-permute-start | bytes 1376264 | tf_op jit(solution)/shard_map/ppermute | solution.py:386
  23.0 34.3 %copy-start = (f32[16,56,1,128]{3,2,1,0:T(1,128)}, f32[16,56,1,128]{3,2,1,0:T(1,128)S(1)}, u32[]{:S(2)}) copy-start(f32[16,56,1,128]{3,2,1,0:T(1,128)S(1)} %collective-permute-done.p1) | copy-start | bytes 1376260
  40.5 16.7 %copy-start.1 = (f32[16,56,1,128]{3,2,1,0:T(1,128)}, f32[16,56,1,128]{3,2,1,0:T(1,128)S(1)}, u32[]{:S(2)}) copy-start(f32[16,56,1,128]{3,2,1,0:T(1,128)S(1)} %collective-permute-done.1.p2) | copy-start | bytes 1376260
  73.8 54.3 %all-to-all-start.1 = ((f32[64,56,1,128]{3,2,1,0:T(1,128)}), f32[64,56,1,128]{3,2,1,0:T(1,128)}, u32[]{:S(2)}, u32[]{:S(2)}) async-start(f32[64,56,1,128]{3,2,1,0:T(1,128)} %get-tuple-element.18), calls=%async_computation.1 | async-start | bytes 3670016 | tf_op jit(solution)/shard_map/all_to_all | solution.py:365
  99.3 1.7 %collective-permute-start.3 = (f32[1188,128]{1,0:T(8,128)}, f32[1188,128]{1,0:T(8,128)S(1)}, u32[]{:S(2)}, u32[]{:S(2)}) collective-permute-start(f32[1188,128]{1,0:T(8,128)} %get-tuple-element.17), channel_id=1, source_target_pairs={{0,0},{1,2},{2,1},{3,3},{4,4},{5,6},{6,5},{7,7},{8,8},{9,10},{10,9... | collective-permute-start | bytes 1824776 | tf_op jit(solution)/shard_map/ppermute | solution.py:391
  101.0 42.0 %collective-permute-start.4 = (f32[1188,128]{1,0:T(8,128)S(1)}, f32[1188,128]{1,0:T(8,128)S(1)}, u32[]{:S(2)}, u32[]{:S(2)}) collective-permute-start(f32[1188,128]{1,0:T(8,128)S(1)} %collective-permute-done.3), channel_id=1, source_target_pairs={{0,0},{2,66},{1,129},{3,195},{4,4},{6,70},{5,133},{7,199},{8,8},{1... | collective-permute-start | bytes 1824776 | tf_op jit(solution)/shard_map/ppermute | solution.py:393
  101.7 41.3 %collective-permute-start.5 = (f32[8,128]{1,0:T(8,128)S(1)}, f32[8,128]{1,0:T(8,128)S(1)}, u32[]{:S(2)}, u32[]{:S(2)}) collective-permute-start(f32[8,128]{1,0:T(8,128)S(1)} %slice.4), channel_id=1, source_target_pairs={{0,1},{1,0},{2,3},{3,2},{4,5},{5,4},{6,7},{7,6},{8,9},{9,8},{10,11... | collective-permute-start | bytes 12296 | tf_op jit(solution)/shard_map/ppermute | solution.py:392
  143.0 0.6 copy-start.2
where the time goes:
time: 147 us; the launch traced here: 144 us
  waiting for transfers between devices  53.6 us (36%)
  starting transfers between devices  45.9 us (31%)
  Pallas kernels  43.6 us (30%)
    ppermute x3, waiting for transfers between devices, per_device(): lax.ppermute(pieces[r], 'lat', [(l, l ^ r) for l in range(4)])  34.2 us
    all_to_all x2, starting transfers between devices, exchanged(): return lax.all_to_all(parts, 'cfg', split_axis=0, concat_axis=0, tiled=True)  20.1 us
    ppermute x1, starting transfers between devices, per_device(): tick = lax.ppermute(sums_a[:SUB], 'lat', [(l, l ^ 1) for l in range(4)])  19.9 us
    all_to_all x2, waiting for transfers between devices, exchanged(): return lax.all_to_all(parts, 'cfg', split_axis=0, concat_axis=0, tiled=True)  19.4 us
    pallas_call x1, Pallas kernels, first_density(): pl.pallas_call(first_kernel, out_shape=(shape((66 * groups, LANES), F32),...  18.5 us
    pallas_call x1, Pallas kernels, second_density(): pl.pallas_call(second_kernel, out_shape=outputs(), in_specs=[VMEM, VMEM,...  14.9 us
    pallas_call x1, Pallas kernels, merge(): pl.pallas_call(merge_kernel, out_shape=(jax.ShapeDtypeStruct((64, rows, 1...  3.61 us
    ppermute x3, starting transfers between devices, per_device(): lax.ppermute(pieces[r], 'lat', [(l, l ^ r) for l in range(4)])  3.44 us
  transfers between devices with their start and end apart: 8, of which 4 were waited for; matrix products, arithmetic and copies ran while one was open for 0% of the time, Pallas kernels for 27%

commit v1 on v0

--- a/solution.py
+++ b/solution.py
@@ -104,20 +104,20 @@
     )(mode[:, :, :, None, :], var[:, :, :, None, :])
 
 
-def merge_kernel(p0, p1, p2, p3, grid_offset, out, offset, held, in_sems, out_sems):
+def merge_kernel(p0, p1, p2, p3, grid_offset, out, offset, held, in_sem, out_sems):
     lat = lax.axis_index("lat")
-    arrive, leave = [], []
-    for r, piece in enumerate((p0, p1, p2, p3)):
+    arrive = pltpu.make_async_copy(p0, held, in_sem.at[0])
+    arrive.start()
+    leave = []
+    for r, piece in enumerate((held, p1, p2, p3)):
         at = pl.ds(16 * jnp.bitwise_xor(lat, r), 16)
-        arrive.append(pltpu.make_async_copy(piece, held.at[r], in_sems.at[r]))
-        leave.append(pltpu.make_async_copy(held.at[r], out.at[at], out_sems.at[r]))
-    for c in arrive:
-        c.start()
+        leave.append(pltpu.make_async_copy(piece, out.at[at], out_sems.at[r]))
+    for go in leave[1:]:
+        go.start()
     for g in range(64):
         offset[g : g + 1, :] = jnp.full((1, LANES), grid_offset[g], F32)
-    for c, go in zip(arrive, leave):
-        c.wait()
-        go.start()
+    arrive.wait()
+    leave[0].start()
     for go in leave:
         go.wait()
 
@@ -127,11 +127,11 @@
     return pl.pallas_call(
         merge_kernel,
         out_shape=(jax.ShapeDtypeStruct((64, rows, 1, LANES), F32), jax.ShapeDtypeStruct((64, LANES), F32)),
-        in_specs=[HBM] * 4 + [SMEM],
+        in_specs=[HBM] + [VMEM] * 3 + [SMEM],
         out_specs=[HBM, VMEM],
         scratch_shapes=[
-            pltpu.VMEM((4, 16, rows, 1, LANES), F32),
-            pltpu.SemaphoreType.DMA((4,)),
+            pltpu.VMEM((16, rows, 1, LANES), F32),
+            pltpu.SemaphoreType.DMA((1,)),
             pltpu.SemaphoreType.DMA((4,)),
         ],
         name="merge",
@@ -384,7 +384,7 @@
     arrived = [pieces[0]]
     for r in range(1, 4):
         arrived.append(lax.ppermute(pieces[r], "lat", [(l, l ^ r) for l in range(4)]))
-    part_b, offset = merge(arrived, grid_offset)
+    part_b, offset = merge([arrived[0]] + [in_vmem(a) for a in arrived[1:]], grid_offset)
     data_b = exchanged(part_b)
     sums_a, norm = first_density(in_vmem(data_a.reshape(-1, LANES)), offset)
     along_x, along_z = way_home()

time: 147 us -> 145 us (0.986)
  the two profiles are of different devices: /device:TPU:2 before, /device:TPU:26 now
where the time goes in v1:
time: 145 us; the launch traced here: 144 us
  waiting for transfers between devices  53.8 us (37%)
  starting transfers between devices  44.9 us (31%)
  Pallas kernels  44.3 us (31%)
    ppermute x3, waiting for transfers between devices, per_device(): lax.ppermute(pieces[r], 'lat', [(l, l ^ r) for l in range(4)])  37.8 us
    all_to_all x2, starting transfers between devices, exchanged(): return lax.all_to_all(parts, 'cfg', split_axis=0, concat_axis=0, tiled=True)  19.9 us
    pallas_call x1, Pallas kernels, first_density(): pl.pallas_call(first_kernel, out_shape=(shape((66 * groups, LANES), F32),...  19.4 us
    ppermute x1, starting transfers between devices, per_device(): tick = lax.ppermute(sums_a[:SUB], 'lat', [(l, l ^ 1) for l in range(4)])  19.2 us
    all_to_all x2, waiting for transfers between devices, exchanged(): return lax.all_to_all(parts, 'cfg', split_axis=0, concat_axis=0, tiled=True)  16 us
    pallas_call x1, Pallas kernels, second_density(): pl.pallas_call(second_kernel, out_shape=outputs(), in_specs=[VMEM, VMEM,...  14.9 us
    ppermute x3, starting transfers between devices, per_device(): lax.ppermute(pieces[r], 'lat', [(l, l ^ r) for l in range(4)])  3.44 us
    pallas_call x1, Pallas kernels, merge(): pl.pallas_call(merge_kernel, out_shape=(jax.ShapeDtypeStruct((64, rows, 1...  3.4 us
  transfers between devices with their start and end apart: 8, of which 4 were waited for; matrix products, arithmetic and copies ran while one was open for 0% of the time, Pallas kernels for 28%

profile of v1, /device:TPU:26, one launch (start us, length us, event | category | flops | bytes accessed | tf_op | source)
XLA Modules:
  0.0 144.4 jit_solution(16101312153297188158)
XLA Ops:
  0.6 3.2 %pack_first.1 = f32[64,73,1,128]{3,2,1,0:T(1,128)} custom-call(f32[16,4,64,1,128]{4,3,2,1,0:T(1,128)} %bitcast.12, f32[16,4,64,1,128]{4,3,2,1,0:T(1,128)} %bitcast.14, f32[2]{0:T(128)} %weight.1), custom_call_target="tpu_custom_call" | custom-call | tf_op jit(solution)/shard_map/pack_first/pallas_call | solution.py:63
  3.9 13.0 %all-to-all-start = ((f32[64,73,1,128]{3,2,1,0:T(1,128)}), f32[64,73,1,128]{3,2,1,0:T(1,128)}, u32[]{:S(2)}, u32[]{:S(2)}) async-start(f32[64,73,1,128]{3,2,1,0:T(1,128)} %pack_first.1), calls=%async_computation | async-start | bytes 4784128 | tf_op jit(solution)/shard_map/all_to_all | solution.py:365
  16.8 2.5 %pack_second.1 = (f32[16,56,1,128]{3,2,1,0:T(1,128)}, f32[16,56,1,128]{3,2,1,0:T(1,128)}, f32[16,56,1,128]{3,2,1,0:T(1,128)}, f32[16,56,1,128]{3,2,1,0:T(1,128)}) custom-call(f32[16,4,64,1,128]{4,3,2,1,0:T(1,128)} %bitcast.13, f32[16,4,64,1,128]{4,3,2,1,0:T(1,128)} %bitcast.15), custom_call_target="tpu_custom_call" | custom-call | tf_op jit(solution)/shard_map/pack_second/pallas_call | solution.py:97
  19.3 0.1 collective-permute-start
  19.4 2.2 %collective-permute-start.1 = (f32[16,56,1,128]{3,2,1,0:T(1,128)}, f32[16,56,1,128]{3,2,1,0:T(1,128)S(1)}, u32[]{:S(2)}, u32[]{:S(2)}) collective-permute-start(f32[16,56,1,128]{3,2,1,0:T(1,128)} %get-tuple-element.14), channel_id=1, source_target_pairs={{0,2},{1,3},{2,0},{3,1},{4,6},{5,7},{6,4},{7,5},{8,10},{9,11},{10,... | collective-permute-start | bytes 1376264 | tf_op jit(solution)/shard_map/ppermute | solution.py:386
  21.6 1.1 collective-permute-start.2
  22.8 0.0 collective-permute-done.p1
  22.8 20.0 %collective-permute-done.1.p2 = f32[16,56,1,128]{3,2,1,0:T(1,128)S(1)} collective-permute-done((f32[16,56,1,128]{3,2,1,0:T(1,128)}, f32[16,56,1,128]{3,2,1,0:T(1,128)S(1)}, u32[]{:S(2)}, u32[]{:S(2)}) %collective-permute-start.1) | collective-permute-done | bytes 458784 | tf_op jit(solution)/shard_map/ppermute | solution.py:386
  42.8 17.8 %collective-permute-done.2.p3 = f32[16,56,1,128]{3,2,1,0:T(1,128)S(1)} collective-permute-done((f32[16,56,1,128]{3,2,1,0:T(1,128)}, f32[16,56,1,128]{3,2,1,0:T(1,128)S(1)}, u32[]{:S(2)}, u32[]{:S(2)}) %collective-permute-start.2) | collective-permute-done | bytes 458784 | tf_op jit(solution)/shard_map/ppermute | solution.py:386
  60.6 3.4 %merge.1 = (f32[64,56,1,128]{3,2,1,0:T(1,128)}, f32[64,128]{1,0:T(8,128)}) custom-call(f32[16,56,1,128]{3,2,1,0:T(1,128)} %get-tuple-element.12.p0, f32[16,56,1,128]{3,2,1,0:T(1,128)S(1)} %collective-permute-done.p1, f32[16,56,1,128]{3,2,1,0:T(1,128)S(1)} %collective-permute-done.1.p2, f32[16,56,1,128]{3,2,1,0:T(1,128)S(1)} %collective-permute-done.2.p3, ...), custom_call_target="tpu_custom_call" | custom-call | tf_op jit(solution)/shard_map/merge/pallas_call | solution.py:127
  64.0 9.5 %all-to-all-done = f32[64,73,1,128]{3,2,1,0:T(1,128)} async-done(((f32[64,73,1,128]{3,2,1,0:T(1,128)}), f32[64,73,1,128]{3,2,1,0:T(1,128)}, u32[]{:S(2)}, u32[]{:S(2)}) %all-to-all-start) | async-done | bytes 2392096 | tf_op jit(solution)/shard_map/all_to_all | solution.py:365
  73.5 7.0 %all-to-all-start.1 = ((f32[64,56,1,128]{3,2,1,0:T(1,128)}), f32[64,56,1,128]{3,2,1,0:T(1,128)}, u32[]{:S(2)}, u32[]{:S(2)}) async-start(f32[64,56,1,128]{3,2,1,0:T(1,128)} %get-tuple-element.18), calls=%async_computation.1 | async-start | bytes 3670016 | tf_op jit(solution)/shard_map/all_to_all | solution.py:365
  80.5 19.4 %first_density.1 = (f32[1188,128]{1,0:T(8,128)}, f32[128,128]{1,0:T(8,128)}) custom-call(f32[4672,128]{1,0:T(8,128)} %bitcast.6.data, f32[64,128]{1,0:T(8,128)} %get-tuple-element.16.offset), custom_call_target="tpu_custom_call" | custom-call | flops 113246208 | bytes 2359296 | tf_op jit(solution)/shard_map/first_density/pallas_call | solution.py:311
  100.0 1.7 %collective-permute-start.3 = (f32[1188,128]{1,0:T(8,128)}, f32[1188,128]{1,0:T(8,128)S(1)}, u32[]{:S(2)}, u32[]{:S(2)}) collective-permute-start(f32[1188,128]{1,0:T(8,128)} %get-tuple-element.17), channel_id=1, source_target_pairs={{0,0},{1,2},{2,1},{3,3},{4,4},{5,6},{6,5},{7,7},{8,8},{9,10},{10,9... | collective-permute-start | bytes 1824776 | tf_op jit(solution)/shard_map/ppermute | solution.py:391
  101.7 0.0 collective-permute-done.3
  101.7 0.7 collective-permute-start.4
  102.4 19.2 %collective-permute-start.5 = (f32[8,128]{1,0:T(8,128)S(1)}, f32[8,128]{1,0:T(8,128)S(1)}, u32[]{:S(2)}, u32[]{:S(2)}) collective-permute-start(f32[8,128]{1,0:T(8,128)S(1)} %slice.4), channel_id=1, source_target_pairs={{0,1},{1,0},{2,3},{3,2},{4,5},{5,4},{6,7},{7,6},{8,9},{9,8},{10,11... | collective-permute-start | bytes 12296 | tf_op jit(solution)/shard_map/ppermute | solution.py:392
  121.5 6.5 %all-to-all-done.1 = f32[64,56,1,128]{3,2,1,0:T(1,128)} async-done(((f32[64,56,1,128]{3,2,1,0:T(1,128)}), f32[64,56,1,128]{3,2,1,0:T(1,128)}, u32[]{:S(2)}, u32[]{:S(2)}) %all-to-all-start.1) | async-done | bytes 1835040 | tf_op jit(solution)/shard_map/all_to_all | solution.py:365
  128.0 14.9 %second_density.1 = (f32[64,4096]{1,0:T(8,128)}, f32[2,4096]{1,0:T(2,128)}) custom-call(f32[3584,128]{1,0:T(8,128)} %bitcast.11.data, f32[64,128]{1,0:T(8,128)} %get-tuple-element.16.offset, f32[128,128]{1,0:T(8,128)} %get-tuple-element.19.norm), custom_call_target="tpu_custom_call" | custom-call | flops 88080384 | bytes 1835008 | tf_op jit(solution)/shard_map/second_density/pallas_call | solution.py:333
  142.9 0.0 collective-permute-done.5.tick
  142.9 0.0 copy-start
  142.9 0.0 collective-permute-done.4.first
  142.9 0.6 copy-done
  143.5 0.9 place.1
  (1 shorter events, 0.0 us)
Async XLA Ops:
  3.9 69.6 %all-to-all-start = ((f32[64,73,1,128]{3,2,1,0:T(1,128)}), f32[64,73,1,128]{3,2,1,0:T(1,128)}, u32[]{:S(2)}, u32[]{:S(2)}) async-start(f32[64,73,1,128]{3,2,1,0:T(1,128)} %pack_first.1), calls=%async_computation | async-start | bytes 4784128 | tf_op jit(solution)/shard_map/all_to_all | solution.py:365
  19.3 3.5 %collective-permute-start = (f32[16,56,1,128]{3,2,1,0:T(1,128)}, f32[16,56,1,128]{3,2,1,0:T(1,128)S(1)}, u32[]{:S(2)}, u32[]{:S(2)}) collective-permute-start(f32[16,56,1,128]{3,2,1,0:T(1,128)} %get-tuple-element.13), channel_id=1, source_target_pairs={{0,1},{1,0},{2,3},{3,2},{4,5},{5,4},{6,7},{7,6},{8,9},{9,8},{10,11... | collective-permute-start | bytes 1376264 | tf_op jit(solution)/shard_map/ppermute | solution.py:386
  19.4 23.4 %collective-permute-start.1 = (f32[16,56,1,128]{3,2,1,0:T(1,128)}, f32[16,56,1,128]{3,2,1,0:T(1,128)S(1)}, u32[]{:S(2)}, u32[]{:S(2)}) collective-permute-start(f32[16,56,1,128]{3,2,1,0:T(1,128)} %get-tuple-element.14), channel_id=1, source_target_pairs={{0,2},{1,3},{2,0},{3,1},{4,6},{5,7},{6,4},{7,5},{8,10},{9,11},{10,... | collective-permute-start | bytes 1376264 | tf_op jit(solution)/shard_map/ppermute | solution.py:386
  21.6 39.0 %collective-permute-start.2 = (f32[16,56,1,128]{3,2,1,0:T(1,128)}, f32[16,56,1,128]{3,2,1,0:T(1,128)S(1)}, u32[]{:S(2)}, u32[]{:S(2)}) collective-permute-start(f32[16,56,1,128]{3,2,1,0:T(1,128)} %get-tuple-element.15), channel_id=1, source_target_pairs={{0,3},{1,2},{2,1},{3,0},{4,7},{5,6},{6,5},{7,4},{8,11},{9,10},{10,... | collective-permute-start | bytes 1376264 | tf_op jit(solution)/shard_map/ppermute | solution.py:386
  73.5 54.5 %all-to-all-start.1 = ((f32[64,56,1,128]{3,2,1,0:T(1,128)}), f32[64,56,1,128]{3,2,1,0:T(1,128)}, u32[]{:S(2)}, u32[]{:S(2)}) async-start(f32[64,56,1,128]{3,2,1,0:T(1,128)} %get-tuple-element.18), calls=%async_computation.1 | async-start | bytes 3670016 | tf_op jit(solution)/shard_map/all_to_all | solution.py:365
  100.0 1.7 %collective-permute-start.3 = (f32[1188,128]{1,0:T(8,128)}, f32[1188,128]{1,0:T(8,128)S(1)}, u32[]{:S(2)}, u32[]{:S(2)}) collective-permute-start(f32[1188,128]{1,0:T(8,128)} %get-tuple-element.17), channel_id=1, source_target_pairs={{0,0},{1,2},{2,1},{3,3},{4,4},{5,6},{6,5},{7,7},{8,8},{9,10},{10,9... | collective-permute-start | bytes 1824776 | tf_op jit(solution)/shard_map/ppermute | solution.py:391
  101.7 41.3 %collective-permute-start.4 = (f32[1188,128]{1,0:T(8,128)S(1)}, f32[1188,128]{1,0:T(8,128)S(1)}, u32[]{:S(2)}, u32[]{:S(2)}) collective-permute-start(f32[1188,128]{1,0:T(8,128)S(1)} %collective-permute-done.3), channel_id=1, source_target_pairs={{0,0},{2,66},{1,129},{3,195},{4,4},{6,70},{5,133},{7,199},{8,8},{1... | collective-permute-start | bytes 1824776 | tf_op jit(solution)/shard_map/ppermute | solution.py:393
  102.4 40.5 %collective-permute-start.5 = (f32[8,128]{1,0:T(8,128)S(1)}, f32[8,128]{1,0:T(8,128)S(1)}, u32[]{:S(2)}, u32[]{:S(2)}) collective-permute-start(f32[8,128]{1,0:T(8,128)S(1)} %slice.4), channel_id=1, source_target_pairs={{0,1},{1,0},{2,3},{3,2},{4,5},{5,4},{6,7},{7,6},{8,9},{9,8},{10,11... | collective-permute-start | bytes 12296 | tf_op jit(solution)/shard_map/ppermute | solution.py:392
  142.9 0.6 copy-start
